TPU v7x, 32 devices: a whole 2x2x4 slice. The times are simulated.
32 devices in a mesh: dp: 8 (over z, x), col: 4 (over y, core).
Axes of the slice: x: 2, y: 2, z: 4, core: 2. Of those that a mesh axis runs over, the one named last changes fastest.
Arguments:
- tokens: bfloat16 [50432, 384], P(('dp', 'col')), may hold values from -40 to 40
- packed: bfloat16 [384, 1152], P('dp', 'col'), may hold values from -0.3125 to 0.3125
- packed_bias: float32 [1152], P('col'), may hold values from -3 to 3
- projection: bfloat16 [384, 384], P('col', 'dp'), may hold values from -2.5 to 2.5
- projection_bias: float32 [384], replicated, may hold values from -3 to 3
- expansion: bfloat16 [384, 1536], P('dp', 'col'), may hold values from -0.3125 to 0.3125
- expansion_bias: float32 [1536], P('col'), may hold values from -3 to 3
- reduction: bfloat16 [1536, 384], P('col', 'dp'), may hold values from -0.15625 to 0.15625
- reduction_bias: float32 [384], replicated, may hold values from -3 to 3
- first_scale: float32 [384], replicated, may hold values from 0.25 to 1.75
- first_shift: float32 [384], replicated, may hold values from -3 to 3
- second_scale: float32 [384], replicated, may hold values from 0.25 to 1.75
- second_shift: float32 [384], replicated, may hold values from -3 to 3
- upstream: bfloat16 [50432, 384], P(('dp', 'col')), may hold values from -6 to 6
Outputs:
- layer_output: bfloat16 [50432, 384], P(('dp', 'col'))
- input_grad: float32 [50432, 384], P(('dp', 'col'))
- packed_grad: float32 [384, 1152], P('dp', 'col')
- projection_grad: float32 [384, 384], P('col', 'dp')
- expansion_grad: float32 [384, 1536], P('dp', 'col')
- reduction_grad: float32 [1536, 384], P('col', 'dp')
- packed_bias_grad: float32 [1152], P('col')
- projection_bias_grad: float32 [384], P('col')
- expansion_bias_grad: float32 [1536], P('col')
- reduction_bias_grad: float32 [384], P('col')
- first_scale_grad: float32 [384], P('col')
- first_shift_grad: float32 [384], P('col')
- second_scale_grad: float32 [384], P('col')
- second_shift_grad: float32 [384], P('col')
All inputs are finite; a program needn't handle non-finite values.
Results may differ from a plain program's by a relative error of at most 0.023.
Values may be sent and summed in bfloat16 or wider, within the bound.
A program may use at most 192 MiB of HBM per device.

v0:
```python
import jax
import jax.numpy as jnp
from jax import lax
from jax.sharding import PartitionSpec as P

D = 384
HEADS = 6
SEQ = 197
epsilon = 1e-06
root_half = 0.7071067811865476
inv_root_tau = 0.3989422804014327


def gelu_slope(values):
    return (
        0.5 * (1.0 + lax.erf(values * root_half))
        + values * jnp.exp(-0.5 * values * values) * inv_root_tau
    )


def contract_rows(left, right):
    return lax.dot_general(
        left, right, (((0,), (0,)), ((), ())), preferred_element_type=jnp.float32
    )


def contract_cols(left, right):
    return lax.dot_general(
        left, right, (((1,), (1,)), ((), ())), preferred_element_type=jnp.float32
    )


def full_rows(values):
    return lax.all_gather(values, "col", axis=0, tiled=True)


def feature_sums(term):
    return lax.psum_scatter(
        term.astype(jnp.bfloat16), "col", scatter_dimension=0, tiled=True
    ).astype(jnp.float32)


def norm_forward(values, scale, shift):
    average = jnp.mean(values, axis=1, keepdims=True)
    meansq = jnp.mean(values * values, axis=1, keepdims=True)
    inverse = lax.rsqrt(meansq - average * average + epsilon)
    normed = (values - average) * inverse
    return (normed, inverse, (normed * scale + shift).astype(jnp.bfloat16))


def norm_backward(upper, normed, inverse, scale):
    scaled = upper * scale
    return inverse * (
        scaled
        - jnp.mean(scaled, axis=1, keepdims=True)
        - normed * jnp.mean(scaled * normed, axis=1, keepdims=True)
    )


def attend_forward(packed_img):
    images = packed_img.shape[0]
    head_dim = D // HEADS
    fields = packed_img.reshape(images, SEQ, 3, HEADS, head_dim)
    scores = jnp.einsum(
        "bqhd,bkhd->bhqk", fields[:, :, 0], fields[:, :, 1], preferred_element_type=jnp.float32
    ) * head_dim ** (-0.5)
    logsum = jnp.log(jnp.sum(jnp.exp(scores), axis=-1))
    prob_rows = jnp.exp(scores - logsum[..., None]).astype(jnp.bfloat16)
    mixed = jnp.einsum(
        "bhqk,bkhd->bqhd", prob_rows, fields[:, :, 2], preferred_element_type=jnp.float32
    )
    return (mixed.astype(jnp.bfloat16).reshape(images, SEQ, D), logsum)


def attend_backward(packed_img, logsum, grad_img):
    images = packed_img.shape[0]
    head_dim = D // HEADS
    factor = head_dim ** (-0.5)
    fields = packed_img.reshape(images, SEQ, 3, HEADS, head_dim)
    query_rows = fields[:, :, 0]
    key_rows = fields[:, :, 1]
    value_rows = fields[:, :, 2]
    grad_heads = grad_img.reshape(images, SEQ, HEADS, head_dim)
    scores = (
        jnp.einsum("bqhd,bkhd->bhqk", query_rows, key_rows, preferred_element_type=jnp.float32)
        * factor
    )
    probs_full = jnp.exp(scores - logsum[..., None])
    prob_rows = probs_full.astype(jnp.bfloat16)
    grad_probs = jnp.einsum(
        "bqhd,bkhd->bhqk", grad_heads, value_rows, preferred_element_type=jnp.float32
    )
    delta = jnp.sum(probs_full * grad_probs, axis=-1, keepdims=True)
    grad_scores = (probs_full * (grad_probs - delta) * factor).astype(jnp.bfloat16)
    grad_query = jnp.einsum(
        "bhqk,bkhd->bqhd", grad_scores, key_rows, preferred_element_type=jnp.float32
    )
    grad_key = jnp.einsum(
        "bhqk,bqhd->bkhd", grad_scores, query_rows, preferred_element_type=jnp.float32
    )
    grad_value = jnp.einsum(
        "bhqk,bqhd->bkhd", prob_rows, grad_heads, preferred_element_type=jnp.float32
    )
    stacked = jnp.stack([grad_query, grad_key, grad_value], axis=2)
    return stacked.reshape(images, SEQ, 3 * D).astype(jnp.bfloat16)


def body(
    tokens,
    packed,
    packed_bias,
    projection,
    projection_bias,
    expansion,
    expansion_bias,
    reduction,
    reduction_bias,
    first_scale,
    first_shift,
    second_scale,
    second_shift,
    upstream,
):
    groups = lax.axis_size("col")
    packed_full, projection_full, expansion_full, reduction_full = (
        lax.all_gather(packed, "dp", axis=0, tiled=True),
        lax.all_gather(projection, "dp", axis=1, tiled=True),
        lax.all_gather(expansion, "dp", axis=0, tiled=True),
        lax.all_gather(reduction, "dp", axis=1, tiled=True),
    )
    tokens_f = tokens.astype(jnp.float32)
    upstream_f = upstream.astype(jnp.float32)
    normed1, inverse1, rows1 = norm_forward(tokens_f, first_scale, first_shift)
    rows1_full = full_rows(rows1)
    count = rows1_full.shape[0]
    images = count // SEQ
    local = images // groups
    packed_rows = (
        jnp.dot(rows1_full, packed_full, preferred_element_type=jnp.float32) + packed_bias
    ).astype(jnp.bfloat16)
    received = lax.all_to_all(
        packed_rows.reshape(groups, local, SEQ, -1), "col", split_axis=0, concat_axis=3, tiled=True
    )
    mixed, logsum_img = attend_forward(received[0])
    scattered_img = lax.all_to_all(mixed[None], "col", split_axis=3, concat_axis=0, tiled=True)
    logsum = logsum_img[None]
    attn_rows = scattered_img.reshape(count, -1)
    resid = (
        tokens_f
        + feature_sums(jnp.dot(attn_rows, projection_full, preferred_element_type=jnp.float32))
        + projection_bias
    )
    normed2, inverse2, rows2 = norm_forward(resid, second_scale, second_shift)
    rows2_full = full_rows(rows2)
    hidden_pre = (
        jnp.dot(rows2_full, expansion_full, preferred_element_type=jnp.float32) + expansion_bias
    )
    hidden_act = jax.nn.gelu(hidden_pre, approximate=False).astype(jnp.bfloat16)
    layer_output = (
        resid
        + (
            feature_sums(jnp.dot(hidden_act, reduction_full, preferred_element_type=jnp.float32))
            + reduction_bias
        )
    ).astype(jnp.bfloat16)
    upstream_full = full_rows(upstream)
    reduction_bias_grad = jnp.sum(upstream_f, axis=0)
    reduction_grad = contract_rows(hidden_act, upstream_full)
    hidden_grad = contract_cols(upstream_full, reduction_full) * gelu_slope(hidden_pre)
    expansion_bias_grad = jnp.sum(hidden_grad, axis=0)
    hidden_grad_b = hidden_grad.astype(jnp.bfloat16)
    expansion_grad = contract_rows(rows2_full, hidden_grad_b)
    rows2_grad = feature_sums(contract_cols(hidden_grad_b, expansion_full))
    second_scale_grad = jnp.sum(rows2_grad * normed2, axis=0)
    second_shift_grad = jnp.sum(rows2_grad, axis=0)
    resid_grad = upstream_f + norm_backward(rows2_grad, normed2, inverse2, second_scale)
    projection_bias_grad = jnp.sum(resid_grad, axis=0)
    resid_grad_b = resid_grad.astype(jnp.bfloat16)
    resid_full = full_rows(resid_grad_b)
    projection_grad = contract_rows(attn_rows, resid_full)
    attn_grad = contract_cols(resid_full, projection_full).astype(jnp.bfloat16)
    grad_img = lax.all_to_all(
        attn_grad.reshape(groups, local, SEQ, -1), "col", split_axis=0, concat_axis=3, tiled=True
    )
    packed_grad_img = attend_backward(received[0], logsum[0], grad_img[0])
    packed_grad_rows = lax.all_to_all(
        packed_grad_img[None], "col", split_axis=3, concat_axis=0, tiled=True
    ).reshape(count, -1)
    packed_bias_grad = jnp.sum(packed_grad_rows.astype(jnp.float32), axis=0)
    packed_grad = contract_rows(rows1_full, packed_grad_rows)
    rows1_grad = feature_sums(contract_cols(packed_grad_rows, packed_full))
    first_scale_grad = jnp.sum(rows1_grad * normed1, axis=0)
    first_shift_grad = jnp.sum(rows1_grad, axis=0)
    input_grad = resid_grad + norm_backward(rows1_grad, normed1, inverse1, first_scale)
    feature_terms = jnp.stack(
        [
            projection_bias_grad,
            reduction_bias_grad,
            first_scale_grad,
            first_shift_grad,
            second_scale_grad,
            second_shift_grad,
        ],
        axis=0,
    )
    shares = lax.psum_scatter(feature_terms, "col", scatter_dimension=1, tiled=True)
    packed_grad, projection_grad, expansion_grad, reduction_grad = (
        lax.psum_scatter(
            packed_grad.astype(jnp.bfloat16), "dp", scatter_dimension=0, tiled=True
        ).astype(jnp.float32),
        lax.psum_scatter(
            projection_grad.astype(jnp.bfloat16), "dp", scatter_dimension=1, tiled=True
        ).astype(jnp.float32),
        lax.psum_scatter(
            expansion_grad.astype(jnp.bfloat16), "dp", scatter_dimension=0, tiled=True
        ).astype(jnp.float32),
        lax.psum_scatter(
            reduction_grad.astype(jnp.bfloat16), "dp", scatter_dimension=1, tiled=True
        ).astype(jnp.float32),
    )
    smalls = lax.psum(
        (
            packed_bias_grad,
            shares[0],
            expansion_bias_grad,
            shares[1],
            shares[2],
            shares[3],
            shares[4],
            shares[5],
        ),
        "dp",
    )
    return (
        layer_output,
        input_grad,
        packed_grad,
        projection_grad,
        expansion_grad,
        reduction_grad,
    ) + tuple(smalls)


def solution(mesh):
    placed = (
        P(("dp", "col"), None),
        P("dp", "col"),
        P("col"),
        P("col", "dp"),
        P(),
        P("dp", "col"),
        P("col"),
        P("col", "dp"),
        P(),
        P(),
        P(),
        P(),
        P(),
        P(("dp", "col"), None),
    )
    return jax.shard_map(
        body,
        mesh=mesh,
        in_specs=placed,
        out_specs=(
            P(("dp", "col"), None),
            P(("dp", "col"), None),
            P("dp", "col"),
            P("col", "dp"),
            P("dp", "col"),
            P("col", "dp"),
            P("col"),
            P("col"),
            P("col"),
            P("col"),
            P("col"),
            P("col"),
            P("col"),
            P("col"),
        ),
        check_vma=False,
    )
```

profile of v0, /device:TPU:0, one launch (start us, length us, event | category | flops | bytes accessed | tf_op | source)
XLA Modules:
  0.0 997.6 jit_solution(13019273879520020617)
XLA Ops:
  12.0 32.6 %all_gather.25 = bf16[384,288]{1,0:T(8,128)(2,1)S(1)} all-gather(bf16[48,288]{1,0:T(8,128)(2,1)S(1)} %copy-done.16), channel_id=1, replica_groups=mesh['dp'=8,'col'=4] {'dp'}, dimensions={0}, use_global_device_ids=true | all-gather | bytes 248832 | tf_op jit(solution)/shard_map/all_gather | solution.py:126
  44.6 8.4 all-gather.5.cloned.1.call-done
  53.0 6.3 fusion.19
  59.3 15.9 %reshape.120 = bf16[4,8,197,288]{2,1,0,3:T(8,128)(2,1)} reshape(bf16[6304,288]{0,1:T(8,128)(2,1)} %fusion.19) | data formatting | bytes 7262208 | tf_op jit(solution)/shard_map/reshape | solution.py:142
  75.2 5.0 copy.77
  80.2 56.5 %all_to_all.60 = bf16[4,8,197,288]{2,3,1,0:T(8,128)(2,1)S(1)} all-to-all(bf16[4,8,197,288]{2,3,1,0:T(8,128)(2,1)S(1)} %copy.77), channel_id=1, replica_groups=mesh['dp'=8,'col'=4] {'col'}, dimensions={0} | all-to-all | bytes 7262208 | tf_op jit(solution)/shard_map/all_to_all | solution.py:141
  139.3 5.3 fusion.83
  144.5 10.6 %fusion.61 = bf16[8,6,64,197]{3,2,1,0:T(8,128)(2,1)S(1)} fusion(bf16[8,197,3,6,64]{1,4,3,2,0:T(8,128)(2,1)} %bitcast.97, f32[8,6,197,197]{2,3,1,0:T(8,128)} %fusion.83), kind=kOutput, calls=%fused_computation.93 | convolution fusion | flops 246508656 | bytes 22444032 | tf_op jit(solution)/shard_map/bhqk,bkhd->bqhd/dot_general | solution.py:69
  160.8 30.9 %all_gather.26 = bf16[96,384]{0,1:T(8,128)(2,1)S(1)} all-gather(bf16[96,48]{0,1:T(8,128)(2,1)S(1)} %copy-done.22), channel_id=1, replica_groups=mesh['dp'=8,'col'=4] {'dp'}, dimensions={1}, use_global_device_ids=true | all-gather | bytes 82944 | tf_op jit(solution)/shard_map/all_gather | solution.py:127
  192.8 5.4 copy.99
  198.3 5.1 copy.85
  210.6 50.5 %reduce-scatter.30.cloned.1.call-done = bf16[1576,384]{1,0:T(8,128)(2,1)} async-done(((bf16[6304,384]{1,0:T(8,128)(2,1)}), bf16[1576,384]{1,0:T(8,128)(2,1)}) %reduce-scatter.30.cloned.1.call-update) | async-done | bytes 1210384
  266.8 31.0 %all_gather.28 = bf16[384,384]{1,0:T(8,128)(2,1)S(1)} all-gather(bf16[48,384]{1,0:T(8,128)(2,1)S(1)} %copy-done.17), channel_id=1, replica_groups=mesh['dp'=8,'col'=4] {'dp'}, dimensions={0}, use_global_device_ids=true | all-gather | bytes 331776 | tf_op jit(solution)/shard_map/all_gather | solution.py:128
  297.8 41.8 %all_gather.29 = bf16[384,384]{0,1:T(8,128)(2,1)S(1)} all-gather(bf16[384,48]{0,1:T(8,128)(2,1)S(1)} %copy-done.18), channel_id=1, replica_groups=mesh['dp'=8,'col'=4] {'dp'}, dimensions={1}, use_global_device_ids=true | all-gather | bytes 331776 | tf_op jit(solution)/shard_map/all_gather | solution.py:129
  339.6 26.5 %fusion.7 = (bf16[6304,384]{1,0:T(8,128)(2,1)}, f32[6304,384]{1,0:T(8,128)}) fusion(f32[384]{0:T(512)S(1)} %copy-done.26, bf16[6304,384]{1,0:T(8,128)(2,1)} %all-gather.7.cloned.1.call-done, bf16[384,384]{1,0:T(8,128)(2,1)S(1)} %all_gather.28), kind=kOutput, calls=%fused_computation.20 | convolution fusion | flops 2018893824 | bytes 19662336 | tf_op jit(solution)/shard_map/dot_general | solution.py:156
  366.1 9.1 fusion.109
  377.3 5.2 convolution_convert_fusion.1
  382.6 7.7 convolution_convert_fusion.2
  390.4 41.5 %reduce-scatter.34.cloned.1.call-done = bf16[1576,384]{1,0:T(8,128)(2,1)} async-done(((bf16[6304,384]{1,0:T(8,128)(2,1)}), bf16[1576,384]{1,0:T(8,128)(2,1)}) %reduce-scatter.34.cloned.1.call-update) | async-done | bytes 1210384
  434.7 48.7 %reduce-scatter.32.cloned.1.call-done = bf16[1576,384]{1,0:T(8,128)(2,1)} async-done(((bf16[6304,384]{1,0:T(8,128)(2,1)}), bf16[1576,384]{1,0:T(8,128)(2,1)}) %reduce-scatter.32.cloned.1.call-update) | async-done | bytes 1210384
  483.5 4.7 fusion.107
  490.8 38.3 %all-gather.11.cloned.1.call-done = bf16[6304,384]{1,0:T(8,128)(2,1)} async-done(((bf16[1576,384]{1,0:T(8,128)(2,1)}), bf16[6304,384]{1,0:T(8,128)(2,1)}) %all-gather.11.cloned.1.call-update) | async-done | bytes 4841488 | tf_op jit(solution)/shard_map/all_gather | solution.py:34
  529.1 4.0 convolution_convert_fusion.4
  533.1 5.6 reshape.122
  545.4 13.2 %fusion.2 = f32[8,6,197,197]{2,3,1,0:T(8,128)} fusion(f32[8,6,197,197]{2,3,1,0:T(8,128)} %fusion.83), kind=kOutput, calls=%fused_computation.8 | output fusion | flops 5598148 | bytes 14902656 | tf_op jit(solution)/shard_map/reduce_sum | solution.py:67
  558.6 6.4 all-to-all-done.2
  566.5 11.7 %fusion.79 = bf16[8,197,1,6,64]{1,4,3,0,2:T(8,128)(2,1)} fusion(bf16[8,197,6,64]{1,3,2,0:T(8,128)(2,1)} %bitcast.105, f32[8,6,197,197]{2,3,1,0:T(8,128)} %fusion.83), kind=kOutput, calls=%fused_computation.102 | convolution fusion | flops 246508656 | bytes 9872064 | tf_op jit(solution)/shard_map/bhqk,bqhd->bkhd/dot_general | solution.py:101
  578.2 6.7 fusion.82
  584.9 16.6 %fusion.76 = bf16[8,197,1,6,64]{1,4,3,0,2:T(8,128)(2,1)} fusion(f32[8,6,197,197]{2,3,1,0:T(8,128)} %fusion.2, f32[8,6,197,197]{2,3,1,0:T(8,128)} %fusion.82, bf16[8,197,3,6,64]{1,4,3,2,0:T(8,128)(2,1)} %bitcast.99), kind=kOutput, calls=%fused_computation.101 | convolution fusion | flops 248371488 | bytes 42104832 | tf_op jit(solution)/shard_map/bhqk,bkhd->bqhd/dot_general | solution.py:95
  601.4 16.9 %fusion.73 = bf16[8,197,1,6,64]{1,4,3,0,2:T(8,128)(2,1)} fusion(f32[8,6,197,197]{2,3,1,0:T(8,128)} %fusion.2, f32[8,6,197,197]{2,3,1,0:T(8,128)} %fusion.82, bf16[8,197,3,6,64]{1,4,3,2,0:T(8,128)(2,1)} %bitcast.100), kind=kOutput, calls=%fused_computation.100 | convolution fusion | flops 248371488 | bytes 42104832 | tf_op jit(solution)/shard_map/bhqk,bqhd->bkhd/dot_general | solution.py:98
  621.5 12.9 %copy.92 = bf16[1,8,197,1152]{2,1,0,3:T(8,128)(2,1)} copy(bf16[1,8,197,1152]{2,3,1,0:T(8,128)(2,1)S(1)} %bitcast.101) | data formatting | bytes 7262208 | tf_op jit(solution)/shard_map/convert_element_type | solution.py:105
  634.4 5.0 all-to-all-start.3
  639.4 7.3 convolution_convert_fusion.5
  647.0 7.3 fusion.84
  654.5 5.1 convolution_convert_fusion.7
  659.6 33.6 %all-to-all-done.3 = bf16[1,8,197,1152]{2,1,0,3:T(8,128)(2,1)} async-done(((bf16[1,8,197,1152]{2,1,0,3:T(8,128)(2,1)}), bf16[1,8,197,1152]{2,1,0,3:T(8,128)(2,1)}, u32[]{:S(2)}, u32[]{:S(2)}) %all-to-all-start.3) | async-done | bytes 3631136 | tf_op jit(solution)/shard_map/all_to_all | solution.py:186
  693.2 12.9 %copy.100 = bf16[1,8,197,4,288]{4,3,1,2,0:T(4,128)(2,1)} copy(bf16[1,8,197,4,288]{2,1,4,3,0:T(8,128)(2,1)} %bitcast.22) | data formatting | bytes 7262208 | tf_op jit(solution)/shard_map/all_to_all | solution.py:186
  706.1 14.4 %copy.94 = bf16[4,1,8,197,288]{3,2,0,4,1:T(8,128)(2,1)} copy(bf16[4,1,8,197,288]{4,0,2,3,1:T(4,128)(2,1)} %bitcast.95) | data formatting | bytes 7262208 | tf_op jit(solution)/shard_map/all_to_all | solution.py:186
  720.5 9.2 reshape.123
  729.7 7.0 convolution_convert_fusion.6
  737.0 7.5 convolution_convert_fusion
  746.0 23.8 %reduce-scatter.24.cloned.1.call-done = bf16[48,384]{1,0:T(8,128)(2,1)} async-done(((bf16[384,384]{1,0:T(8,128)(2,1)}), bf16[48,384]{1,0:T(8,128)(2,1)}) %reduce-scatter.24.cloned.1.call-update) | async-done | bytes 36880 | tf_op jit(solution)/shard_map/reduce_scatter | solution.py:214
  771.2 59.5 %reduce-scatter.22.cloned.1.call-done = bf16[96,48]{0,1:T(8,128)(2,1)} async-done(((bf16[96,384]{0,1:T(8,128)(2,1)}), bf16[96,48]{0,1:T(8,128)(2,1)}) %reduce-scatter.22.cloned.1.call-update) | async-done | bytes 9232 | tf_op jit(solution)/shard_map/reduce_scatter | solution.py:211
  832.0 4.6 convert_reduce_fusion
  836.7 56.0 %reduce-scatter.20.cloned.1.call-done = bf16[48,288]{1,0:T(8,128)(2,1)} async-done(((bf16[384,288]{1,0:T(8,128)(2,1)}), bf16[48,288]{1,0:T(8,128)(2,1)}) %reduce-scatter.20.cloned.1.call-update) | async-done | bytes 27664 | tf_op jit(solution)/shard_map/reduce_scatter | solution.py:208
  894.0 49.1 %reduce-scatter.36.cloned.1.call-done = bf16[1576,384]{1,0:T(8,128)(2,1)} async-done(((bf16[6304,384]{1,0:T(8,128)(2,1)}), bf16[1576,384]{1,0:T(8,128)(2,1)}) %reduce-scatter.36.cloned.1.call-update) | async-done | bytes 1210384
  950.5 16.3 %reduce-scatter.28.cloned.1.call-done = f32[96,6]{1,0:T(8,128)} async-done(((f32[384,6]{1,0:T(8,128)}), f32[96,6]{1,0:T(8,128)}) %reduce-scatter.28.cloned.1.call-update) | async-done | bytes 2320
  968.4 22.2 %all-reduce.4 = (f32[288]{0:T(512)}, f32[96]{0:T(128)}, f32[384]{0:T(512)}, f32[96]{0:T(128)}, f32[96]{0:T(128)}, /*index=5*/f32[96]{0:T(128)}, f32[96]{0:T(128)}, f32[96]{0:T(128)}) all-reduce(f32[288]{0:T(512)S(1)} %convert_reduce_fusion, f32[96]{0:T(128)S(1)} %bitcast.115, ...), channel_id=1, replica_groups=mesh['dp'=8,'col'=4] {'dp'}, use_global_device_ids=true, to_apply=%region_19.0 | all-reduce | flops 1248 | bytes 9984 | tf_op jit(solution)/shard_map/psum | solution.py:221
  (126 shorter events, 61.2 us)
Async XLA Ops:
  7.2 4.8 copy-start.16
  7.2 45.8 %copy-start.25 = (f32[288]{0:T(512)S(1)}, f32[288]{0:T(512)}, u32[]{:S(2)}) copy-start(f32[288]{0:T(512)} %param.16) | copy-start | bytes 3460
  7.2 45.8 %all-gather.5.cloned.1.call-start = ((), (), s32[]{:S(2)}) async-start(), calls=%async_computation.13 | async-start | bytes 6051840 | tf_op jit(solution)/shard_map/all_gather | solution.py:34
  9.1 2.9 copy-start.12
  9.1 2.9 copy-start.14
  44.6 14.7 %copy-start.10 = (bf16[384,288]{1,0:T(8,128)(2,1)}, bf16[384,288]{1,0:T(8,128)(2,1)S(1)}, u32[]{:S(2)}) copy-start(bf16[384,288]{1,0:T(8,128)(2,1)S(1)} %all_gather.25) | copy-start | bytes 663556
  137.2 2.1 copy-start.4
  155.1 5.7 copy-start.22
  157.1 34.6 %all-to-all-start.1 = ((bf16[1,8,197,384]{2,1,0,3:T(8,128)(2,1)}), bf16[1,8,197,384]{2,1,0,3:T(8,128)(2,1)S(1)}, u32[]{:S(2)}, u32[]{:S(2)}) async-start(bf16[1,8,197,384]{2,1,0,3:T(8,128)(2,1)} %copy.83), calls=%async_computation.1 | async-start | bytes 3145728 | tf_op jit(solution)/shard_map/all_to_all | solution.py:145
  160.7 100.4 %reduce-scatter.30.cloned.1.call-start = ((), (), s32[]{:S(2)}) async-start(), calls=%async_computation.22 | async-start | bytes 6051840
  191.7 1.1 copy-start.7
  206.7 3.8 copy-start.5
  210.5 50.6 %copy-start = (bf16[1576,384]{1,0:T(8,128)(2,1)S(1)}, bf16[1576,384]{1,0:T(8,128)(2,1)}, u32[]{:S(2)}) copy-start(bf16[1576,384]{1,0:T(8,128)(2,1)} %param.14) | copy-start | bytes 3631108
  210.5 50.6 %copy-start.19 = (f32[384]{0:T(512)S(1)}, f32[384]{0:T(512)}, u32[]{:S(2)}) copy-start(f32[384]{0:T(512)} %param.18) | copy-start | bytes 4612
  210.5 52.6 %copy-start.20 = (f32[384]{0:T(512)S(1)}, f32[384]{0:T(512)}, u32[]{:S(2)}) copy-start(f32[384]{0:T(512)} %param.25) | copy-start | bytes 4612
  210.5 52.6 %copy-start.23 = (f32[384]{0:T(512)S(1)}, f32[384]{0:T(512)}, u32[]{:S(2)}) copy-start(f32[384]{0:T(512)} %param.26) | copy-start | bytes 4612
  210.6 56.2 %copy-start.17 = (bf16[48,384]{1,0:T(8,128)(2,1)S(1)}, bf16[48,384]{1,0:T(8,128)(2,1)}, u32[]{:S(2)}) copy-start(bf16[48,384]{1,0:T(8,128)(2,1)} %param.19) | copy-start | bytes 110596
  210.6 87.2 %copy-start.18 = (bf16[384,48]{0,1:T(8,128)(2,1)S(1)}, bf16[384,48]{0,1:T(8,128)(2,1)}, u32[]{:S(2)}) copy-start(bf16[384,48]{0,1:T(8,128)(2,1)} %param.21) | copy-start | bytes 110596
  210.6 129.0 %copy-start.26 = (f32[384]{0:T(512)S(1)}, f32[384]{0:T(512)}, u32[]{:S(2)}) copy-start(f32[384]{0:T(512)} %param.20) | copy-start | bytes 4612
  210.6 129.0 %all-gather.7.cloned.1.call-start = ((), (), s32[]{:S(2)}) async-start(), calls=%async_computation.14 | async-start | bytes 6051840 | tf_op jit(solution)/shard_map/all_gather | solution.py:34
  266.2 99.9 %all-gather.9.cloned.1.call-start = ((), (), s32[]{:S(2)}) async-start(), calls=%async_computation.15 | async-start | bytes 6051840 | tf_op jit(solution)/shard_map/all_gather | solution.py:34
  266.7 165.2 %reduce-scatter.34.cloned.1.call-start = ((), (), s32[]{:S(2)}) async-start(), calls=%async_computation.24 | async-start | bytes 6051840
  375.2 2.2 copy-start.1
  382.6 100.9 %reduce-scatter.32.cloned.1.call-start = ((), (), s32[]{:S(2)}) async-start(), calls=%async_computation.23 | async-start | bytes 6051840
  390.3 41.6 %copy-start.3 = (bf16[1576,384]{1,0:T(8,128)(2,1)S(1)}, bf16[1576,384]{1,0:T(8,128)(2,1)}, u32[]{:S(2)}) copy-start(bf16[1576,384]{1,0:T(8,128)(2,1)} %reduce-scatter.30.cloned.1.call-done) | copy-start | bytes 3631108
  390.3 93.2 %copy-start.24 = (f32[384]{0:T(512)S(1)}, f32[384]{0:T(512)}, u32[]{:S(2)}) copy-start(f32[384]{0:T(512)} %param.22) | copy-start | bytes 4612
  390.3 138.8 %all-gather.11.cloned.1.call-start = ((), (), s32[]{:S(2)}) async-start(), calls=%async_computation.16 | async-start | bytes 6051840 | tf_op jit(solution)/shard_map/all_gather | solution.py:34
  488.1 1.4 copy-start.2
  541.4 23.6 %all-to-all-start.2 = ((bf16[4,8,197,96]{2,1,3,0:T(8,128)(2,1)}), bf16[4,8,197,96]{2,1,3,0:T(8,128)(2,1)S(1)}, u32[]{:S(2)}, u32[]{:S(2)}) async-start(bf16[4,8,197,96]{2,1,3,0:T(8,128)(2,1)} %copy.86), calls=%async_computation.2 | async-start | bytes 3145728 | tf_op jit(solution)/shard_map/all_to_all | solution.py:182
  566.5 11.7 %copy-start.8 = (bf16[1,8,197,4,96]{2,4,3,1,0:T(8,128)(2,1)S(1)}, bf16[1,8,197,4,96]{2,4,3,1,0:T(8,128)(2,1)}, u32[]{:S(2)}) copy-start(bf16[1,8,197,4,96]{2,4,3,1,0:T(8,128)(2,1)} %copy.87) | copy-start | bytes 3631108
  601.4 16.9 %copy-start.9 = (bf16[8,197,1,6,64]{1,4,3,0,2:T(8,128)(2,1)S(1)}, bf16[8,197,1,6,64]{1,4,3,0,2:T(8,128)(2,1)}, u32[]{:S(2)}) copy-start(bf16[8,197,1,6,64]{1,4,3,0,2:T(8,128)(2,1)} %fusion.79) | copy-start | bytes 3631108
  634.4 58.8 %all-to-all-start.3 = ((bf16[1,8,197,1152]{2,1,0,3:T(8,128)(2,1)}), bf16[1,8,197,1152]{2,1,0,3:T(8,128)(2,1)}, u32[]{:S(2)}, u32[]{:S(2)}) async-start(bf16[1,8,197,1152]{2,1,0,3:T(8,128)(2,1)} %copy.92), calls=%async_computation.3 | async-start | bytes 9437184 | tf_op jit(solution)/shard_map/all_to_all | solution.py:186
  639.4 105.2 %reduce-scatter.26.cloned.1.call-start = ((), (), s32[]{:S(2)}) async-start(), calls=%async_computation.20 | async-start | bytes 331776 | tf_op jit(solution)/shard_map/reduce_scatter | solution.py:217
  646.8 7.7 copy-start.6
  646.8 123.0 %reduce-scatter.24.cloned.1.call-start = ((), (), s32[]{:S(2)}) async-start(), calls=%async_computation.19 | async-start | bytes 331776 | tf_op jit(solution)/shard_map/reduce_scatter | solution.py:214
  654.4 176.3 %reduce-scatter.22.cloned.1.call-start = ((), (), s32[]{:S(2)}) async-start(), calls=%async_computation.18 | async-start | bytes 110592 | tf_op jit(solution)/shard_map/reduce_scatter | solution.py:211
  659.6 233.1 %reduce-scatter.20.cloned.1.call-start = ((), (), s32[]{:S(2)}) async-start(), calls=%async_computation.17 | async-start | bytes 331776 | tf_op jit(solution)/shard_map/reduce_scatter | solution.py:208
  729.7 7.4 copy-start.11
  736.7 206.5 %reduce-scatter.36.cloned.1.call-start = ((), (), s32[]{:S(2)}) async-start(), calls=%async_computation.25 | async-start | bytes 6051840
  744.5 198.7 %copy-start.13 = (f32[1576]{0:T(1024)S(1)}, f32[1576]{0:T(1024)}, u32[]{:S(2)}) copy-start(f32[1576]{0:T(1024)} %copy-done.12) | copy-start | bytes 18916
  744.5 198.7 %copy-start.15 = (f32[1576]{0:T(1024)S(1)}, f32[1576]{0:T(1024)}, u32[]{:S(2)}) copy-start(f32[1576]{0:T(1024)} %copy-done.14) | copy-start | bytes 18916
  744.5 198.7 %copy-start.21 = (f32[384]{0:T(512)S(1)}, f32[384]{0:T(512)}, u32[]{:S(2)}) copy-start(f32[384]{0:T(512)} %param.23) | copy-start | bytes 4612
  744.5 222.2 %reduce-scatter.28.cloned.1.call-start = ((), (), s32[]{:S(2)}) async-start(), calls=%async_computation.21 | async-start | bytes 245760
Sparse Core Ops, SparseCore 0:
  12.1 40.8 all-gather.4
  210.7 50.3 reduce-scatter.29
  266.3 38.1 all-gather.6
  305.8 38.1 all-gather.8
  382.7 49.1 reduce-scatter.33
  434.4 49.0 reduce-scatter.31
  490.9 38.1 all-gather.10
  646.9 60.9 reduce-scatter.25
  711.2 58.5 reduce-scatter.23
  772.9 57.7 reduce-scatter.21
  834.0 58.5 reduce-scatter.19
  895.1 48.0 reduce-scatter.35
  946.9 19.7 reduce-scatter.27
where the time goes:
time: 1010 us; the launch traced here: 998 us
  waiting for transfers between devices  433 us (43%)
  blocking collectives  215 us (21%)
  matrix products  164 us (16%)
  local copies, waits for them, and re-layouts  106 us (10%)
  other arithmetic  50.6 us (5%)
  between operations  14.7 us (1%)
  starting transfers between devices  13.5 us (1%)
    unnamed x18, waiting for transfers between devices  207 us
    reduce_scatter x1, waiting for transfers between devices, body(): lax.psum_scatter(projection_grad.astype(jnp.bfloat16), 'dp', scatter_dime...  59.5 us
    all_to_all x1, blocking collectives, body(): lax.all_to_all(packed_rows.reshape(groups, local, SEQ, -1), 'col', split_...  56.5 us
    reduce_scatter x1, waiting for transfers between devices, body(): lax.psum_scatter(packed_grad.astype(jnp.bfloat16), 'dp', scatter_dimensio...  56 us
    all_gather x4, waiting for transfers between devices, full_rows(): return lax.all_gather(values, 'col', axis=0, tiled=True)  46.7 us
    all_gather x1, blocking collectives, body(): lax.all_gather(reduction, 'dp', axis=1, tiled=True)  41.8 us
    all_to_all x1, waiting for transfers between devices, body(): lax.all_to_all(packed_grad_img[None], 'col', split_axis=3, concat_axis=0,...  33.6 us
    all_gather x1, blocking collectives, body(): lax.all_gather(packed, 'dp', axis=0, tiled=True)  32.6 us
  transfers between devices with their start and end apart: 16, of which 12 were waited for; matrix products, arithmetic and copies ran while one was open for 14% of the time, Pallas kernels for 0%

commit v1 on v0

--- a/solution.py
+++ b/solution.py
@@ -9,6 +9,29 @@
 epsilon = 1e-06
 root_half = 0.7071067811865476
 inv_root_tau = 0.3989422804014327
+
+
+def cut_along(x, dim, size):
+    before, after = (x.shape[:dim], x.shape[dim + 1 :])
+    return jnp.moveaxis(x.reshape(*before, size, -1, *after), dim, 0)
+
+
+def joined_along(tiles, dim):
+    tiles = jnp.moveaxis(tiles, 0, dim)
+    shape = tiles.shape
+    return tiles.reshape(*shape[:dim], shape[dim] * shape[dim + 1], *shape[dim + 2 :])
+
+
+def exchange_directly(shard, axis, split_dim, concat_dim):
+    length, index = (lax.axis_size(axis), lax.axis_index(axis))
+    pieces = cut_along(shard, split_dim, length)
+    filled = pieces
+    for turn in range(1, length):
+        target, source = ((index + turn) % length, (index - turn) % length)
+        sent = lax.dynamic_index_in_dim(pieces, target, 0)
+        partner_block = lax.ppermute(sent, axis, [(i, (i + turn) % length) for i in range(length)])
+        filled = lax.dynamic_update_slice_in_dim(filled, partner_block, source, axis=0)
+    return joined_along(filled, concat_dim)
 
 
 def gelu_slope(values):
@@ -138,9 +161,7 @@
     packed_rows = (
         jnp.dot(rows1_full, packed_full, preferred_element_type=jnp.float32) + packed_bias
     ).astype(jnp.bfloat16)
-    received = lax.all_to_all(
-        packed_rows.reshape(groups, local, SEQ, -1), "col", split_axis=0, concat_axis=3, tiled=True
-    )
+    received = exchange_directly(packed_rows.reshape(groups, local, SEQ, -1), "col", 0, 3)
     mixed, logsum_img = attend_forward(received[0])
     scattered_img = lax.all_to_all(mixed[None], "col", split_axis=3, concat_axis=0, tiled=True)
     logsum = logsum_img[None]

time: 1010 us -> 1010 us (level)
  blocking collectives: 215 us -> 159 us
  waiting for transfers between devices: 433 us -> 479 us
    all_to_all x1 -> x0, blocking collectives: 56.5 us -> none  [body(): lax.all_to_all(packed_rows.reshape(groups, local, SEQ, -1), 'col', split_...]
    ppermute x0 -> x3, waiting for transfers between devices: none -> 46.2 us  [exchange_directly(): lax.ppermute(sent, axis, [(i, (i + turn) % length) for i in range(length)])]
    another operation x0 -> x2, local copies, waits for them, and re-layouts: none -> 20.9 us  [cut_along(): return jnp.moveaxis(x.reshape(*before, size, -1, *after), dim, 0)]
    reshape x2 -> x0, local copies, waits for them, and re-layouts: 20.9 us -> none  [body(): packed_rows.reshape(groups, local, SEQ, -1)]
  transfers between devices with their start and end apart: 16 -> 19, of which waited for: 12 -> 14; matrix products, arithmetic and copies ran while one was open for 14% -> 14% of each run, Pallas kernels for 0% -> 0%
where the time goes in v1:
time: 1010 us; the launch traced here: 997 us
  waiting for transfers between devices  479 us (47%)
  matrix products  166 us (16%)
  blocking collectives  159 us (16%)
  local copies, waits for them, and re-layouts  113 us (11%)
  other arithmetic  50.6 us (5%)
  starting transfers between devices  15.5 us (2%)
  between operations  14.8 us (1%)
    unnamed x18, waiting for transfers between devices  207 us
    reduce_scatter x1, waiting for transfers between devices, body(): lax.psum_scatter(projection_grad.astype(jnp.bfloat16), 'dp', scatter_dime...  59.5 us
    reduce_scatter x1, waiting for transfers between devices, body(): lax.psum_scatter(packed_grad.astype(jnp.bfloat16), 'dp', scatter_dimensio...  55.9 us
    all_gather x4, waiting for transfers between devices, full_rows(): return lax.all_gather(values, 'col', axis=0, tiled=True)  46.6 us
    ppermute x3, waiting for transfers between devices, exchange_directly(): lax.ppermute(sent, axis, [(i, (i + turn) % length) for i in range(length)])  46.2 us
    all_gather x1, blocking collectives, body(): lax.all_gather(reduction, 'dp', axis=1, tiled=True)  41.8 us
    all_to_all x1, waiting for transfers between devices, body(): lax.all_to_all(packed_grad_img[None], 'col', split_axis=3, concat_axis=0,...  33.6 us
    all_gather x1, blocking collectives, body(): lax.all_gather(packed, 'dp', axis=0, tiled=True)  32.6 us
  transfers between devices with their start and end apart: 19, of which 14 were waited for; matrix products, arithmetic and copies ran while one was open for 14% of the time, Pallas kernels for 0%

profile of v1, /device:TPU:0, one launch (start us, length us, event | category | flops | bytes accessed | tf_op | source)
XLA Modules:
  0.0 997.3 jit_solution(9960602967597587970)
XLA Ops:
  12.1 32.6 %all_gather.25 = bf16[384,288]{1,0:T(8,128)(2,1)S(1)} all-gather(bf16[48,288]{1,0:T(8,128)(2,1)S(1)} %copy-done.16), channel_id=1, replica_groups=mesh['dp'=8,'col'=4] {'dp'}, dimensions={0}, use_global_device_ids=true | all-gather | bytes 248832 | tf_op jit(solution)/shard_map/all_gather | solution.py:149
  44.7 8.3 all-gather.5.cloned.1.call-done
  53.0 6.3 fusion.19
  59.3 15.9 %reshape_reshape.3 = bf16[4,1,8,197,288]{3,2,0,4,1:T(8,128)(2,1)} reshape(bf16[6304,288]{0,1:T(8,128)(2,1)} %fusion.19) | data formatting | bytes 7262208 | tf_op jit(solution)/shard_map/reshape;reshape | solution.py:16
  75.2 5.0 copy.86
  86.3 25.8 %collective-permute-done = bf16[1,1,8,197,288]{3,4,0,2,1:T(8,128)(2,1)} collective-permute-done((bf16[1,1,8,197,288]{3,4,0,2,1:T(8,128)(2,1)}, bf16[1,1,8,197,288]{3,4,0,2,1:T(8,128)(2,1)}, u32[]{:S(2)}, u32[]{:S(2)}) %collective-permute-start) | collective-permute-done | bytes 907808 | tf_op jit(solution)/shard_map/ppermute | solution.py:32
  115.6 20.4 %collective-permute-done.2 = bf16[1,1,8,197,288]{3,4,0,2,1:T(8,128)(2,1)S(1)} collective-permute-done((bf16[1,1,8,197,288]{3,4,0,2,1:T(8,128)(2,1)}, bf16[1,1,8,197,288]{3,4,0,2,1:T(8,128)(2,1)S(1)}, u32[]{:S(2)}, u32[]{:S(2)}) %collective-permute-start.2) | collective-permute-done | bytes 907808 | tf_op jit(solution)/shard_map/ppermute | solution.py:32
  137.1 7.2 fusion.83
  144.3 10.6 %fusion.61 = bf16[8,6,64,197]{3,2,1,0:T(8,128)(2,1)S(1)} fusion(bf16[8,197,3,6,64]{1,4,3,2,0:T(8,128)(2,1)} %bitcast.95, f32[8,6,197,197]{2,3,1,0:T(8,128)} %fusion.83), kind=kOutput, calls=%fused_computation.93 | convolution fusion | flops 246508656 | bytes 22444032 | tf_op jit(solution)/shard_map/bhqk,bkhd->bqhd/dot_general | solution.py:92
  160.5 31.1 %all_gather.26 = bf16[96,384]{0,1:T(8,128)(2,1)S(1)} all-gather(bf16[96,48]{0,1:T(8,128)(2,1)S(1)} %copy-done.22), channel_id=1, replica_groups=mesh['dp'=8,'col'=4] {'dp'}, dimensions={1}, use_global_device_ids=true | all-gather | bytes 82944 | tf_op jit(solution)/shard_map/all_gather | solution.py:150
  192.8 5.4 copy.109
  198.2 5.1 copy.95
  210.6 50.4 %reduce-scatter.30.cloned.1.call-done = bf16[1576,384]{1,0:T(8,128)(2,1)} async-done(((bf16[6304,384]{1,0:T(8,128)(2,1)}), bf16[1576,384]{1,0:T(8,128)(2,1)}) %reduce-scatter.30.cloned.1.call-update) | async-done | bytes 1210384
  266.7 31.0 %all_gather.28 = bf16[384,384]{1,0:T(8,128)(2,1)S(1)} all-gather(bf16[48,384]{1,0:T(8,128)(2,1)S(1)} %copy-done.17), channel_id=1, replica_groups=mesh['dp'=8,'col'=4] {'dp'}, dimensions={0}, use_global_device_ids=true | all-gather | bytes 331776 | tf_op jit(solution)/shard_map/all_gather | solution.py:151
  297.7 41.8 %all_gather.29 = bf16[384,384]{0,1:T(8,128)(2,1)S(1)} all-gather(bf16[384,48]{0,1:T(8,128)(2,1)S(1)} %copy-done.18), channel_id=1, replica_groups=mesh['dp'=8,'col'=4] {'dp'}, dimensions={1}, use_global_device_ids=true | all-gather | bytes 331776 | tf_op jit(solution)/shard_map/all_gather | solution.py:152
  339.5 26.5 %fusion.7 = (bf16[6304,384]{1,0:T(8,128)(2,1)}, f32[6304,384]{1,0:T(8,128)}) fusion(f32[384]{0:T(512)S(1)} %copy-done.26, bf16[6304,384]{1,0:T(8,128)(2,1)} %all-gather.7.cloned.1.call-done, bf16[384,384]{1,0:T(8,128)(2,1)S(1)} %all_gather.28), kind=kOutput, calls=%fused_computation.20 | convolution fusion | flops 2018893824 | bytes 19662336 | tf_op jit(solution)/shard_map/dot_general | solution.py:177
  366.0 9.1 fusion.109
  377.3 5.2 convolution_convert_fusion.1
  382.6 7.7 convolution_convert_fusion.2
  390.4 41.5 %reduce-scatter.34.cloned.1.call-done = bf16[1576,384]{1,0:T(8,128)(2,1)} async-done(((bf16[6304,384]{1,0:T(8,128)(2,1)}), bf16[1576,384]{1,0:T(8,128)(2,1)}) %reduce-scatter.34.cloned.1.call-update) | async-done | bytes 1210384
  434.7 48.7 %reduce-scatter.32.cloned.1.call-done = bf16[1576,384]{1,0:T(8,128)(2,1)} async-done(((bf16[6304,384]{1,0:T(8,128)(2,1)}), bf16[1576,384]{1,0:T(8,128)(2,1)}) %reduce-scatter.32.cloned.1.call-update) | async-done | bytes 1210384
  483.4 4.7 fusion.107
  490.7 38.3 %all-gather.11.cloned.1.call-done = bf16[6304,384]{1,0:T(8,128)(2,1)} async-done(((bf16[1576,384]{1,0:T(8,128)(2,1)}), bf16[6304,384]{1,0:T(8,128)(2,1)}) %all-gather.11.cloned.1.call-update) | async-done | bytes 4841488 | tf_op jit(solution)/shard_map/all_gather | solution.py:57
  533.0 5.6 reshape.117
  545.3 13.2 %fusion.2 = f32[8,6,197,197]{2,3,1,0:T(8,128)} fusion(f32[8,6,197,197]{2,3,1,0:T(8,128)} %fusion.83), kind=kOutput, calls=%fused_computation.8 | output fusion | flops 5598148 | bytes 14902656 | tf_op jit(solution)/shard_map/reduce_sum | solution.py:90
  558.5 6.4 all-to-all-done.1
  566.4 11.7 %fusion.79 = bf16[8,197,1,6,64]{1,4,3,0,2:T(8,128)(2,1)} fusion(bf16[8,197,6,64]{1,3,2,0:T(8,128)(2,1)} %bitcast.103, f32[8,6,197,197]{2,3,1,0:T(8,128)} %fusion.83), kind=kOutput, calls=%fused_computation.102 | convolution fusion | flops 246508656 | bytes 9872064 | tf_op jit(solution)/shard_map/bhqk,bqhd->bkhd/dot_general | solution.py:124
  578.1 6.7 fusion.82
  584.8 16.6 %fusion.76 = bf16[8,197,1,6,64]{1,4,3,0,2:T(8,128)(2,1)} fusion(f32[8,6,197,197]{2,3,1,0:T(8,128)} %fusion.2, f32[8,6,197,197]{2,3,1,0:T(8,128)} %fusion.82, bf16[8,197,3,6,64]{1,4,3,2,0:T(8,128)(2,1)} %bitcast.97), kind=kOutput, calls=%fused_computation.101 | convolution fusion | flops 248371488 | bytes 42104832 | tf_op jit(solution)/shard_map/bhqk,bkhd->bqhd/dot_general | solution.py:118
  601.3 16.9 %fusion.73 = bf16[8,197,1,6,64]{1,4,3,0,2:T(8,128)(2,1)} fusion(f32[8,6,197,197]{2,3,1,0:T(8,128)} %fusion.2, f32[8,6,197,197]{2,3,1,0:T(8,128)} %fusion.82, bf16[8,197,3,6,64]{1,4,3,2,0:T(8,128)(2,1)} %bitcast.98), kind=kOutput, calls=%fused_computation.100 | convolution fusion | flops 248371488 | bytes 42104832 | tf_op jit(solution)/shard_map/bhqk,bqhd->bkhd/dot_general | solution.py:121
  621.4 12.9 %copy.102 = bf16[1,8,197,1152]{2,1,0,3:T(8,128)(2,1)} copy(bf16[1,8,197,1152]{2,3,1,0:T(8,128)(2,1)S(1)} %bitcast.99) | data formatting | bytes 7262208 | tf_op jit(solution)/shard_map/convert_element_type | solution.py:128
  634.3 5.0 all-to-all-start.2
  639.3 7.3 convolution_convert_fusion.5
  646.9 7.3 fusion.84
  654.4 5.1 convolution_convert_fusion.7
  659.5 33.6 %all-to-all-done.2 = bf16[1,8,197,1152]{2,1,0,3:T(8,128)(2,1)} async-done(((bf16[1,8,197,1152]{2,1,0,3:T(8,128)(2,1)}), bf16[1,8,197,1152]{2,1,0,3:T(8,128)(2,1)}, u32[]{:S(2)}, u32[]{:S(2)}) %all-to-all-start.2) | async-done | bytes 3631136 | tf_op jit(solution)/shard_map/all_to_all | solution.py:207
  693.1 12.9 %copy.110 = bf16[1,8,197,4,288]{4,3,1,2,0:T(4,128)(2,1)} copy(bf16[1,8,197,4,288]{2,1,4,3,0:T(8,128)(2,1)} %bitcast.20) | data formatting | bytes 7262208 | tf_op jit(solution)/shard_map/all_to_all | solution.py:207
  706.0 14.4 %copy.104 = bf16[4,1,8,197,288]{3,2,0,4,1:T(8,128)(2,1)} copy(bf16[4,1,8,197,288]{4,0,2,3,1:T(4,128)(2,1)} %bitcast.93) | data formatting | bytes 7262208 | tf_op jit(solution)/shard_map/all_to_all | solution.py:207
  720.4 9.2 reshape.118
  729.6 7.0 convolution_convert_fusion.6
  736.9 7.5 convolution_convert_fusion
  745.9 23.6 %reduce-scatter.24.cloned.1.call-done = bf16[48,384]{1,0:T(8,128)(2,1)} async-done(((bf16[384,384]{1,0:T(8,128)(2,1)}), bf16[48,384]{1,0:T(8,128)(2,1)}) %reduce-scatter.24.cloned.1.call-update) | async-done | bytes 36880 | tf_op jit(solution)/shard_map/reduce_scatter | solution.py:235
  771.0 59.5 %reduce-scatter.22.cloned.1.call-done = bf16[96,48]{0,1:T(8,128)(2,1)} async-done(((bf16[96,384]{0,1:T(8,128)(2,1)}), bf16[96,48]{0,1:T(8,128)(2,1)}) %reduce-scatter.22.cloned.1.call-update) | async-done | bytes 9232 | tf_op jit(solution)/shard_map/reduce_scatter | solution.py:232
  831.8 4.6 convert_reduce_fusion
  836.4 55.9 %reduce-scatter.20.cloned.1.call-done = bf16[48,288]{1,0:T(8,128)(2,1)} async-done(((bf16[384,288]{1,0:T(8,128)(2,1)}), bf16[48,288]{1,0:T(8,128)(2,1)}) %reduce-scatter.20.cloned.1.call-update) | async-done | bytes 27664 | tf_op jit(solution)/shard_map/reduce_scatter | solution.py:229
  893.7 49.2 %reduce-scatter.36.cloned.1.call-done = bf16[1576,384]{1,0:T(8,128)(2,1)} async-done(((bf16[6304,384]{1,0:T(8,128)(2,1)}), bf16[1576,384]{1,0:T(8,128)(2,1)}) %reduce-scatter.36.cloned.1.call-update) | async-done | bytes 1210384
  950.2 16.2 %reduce-scatter.28.cloned.1.call-done = f32[96,6]{1,0:T(8,128)} async-done(((f32[384,6]{1,0:T(8,128)}), f32[96,6]{1,0:T(8,128)}) %reduce-scatter.28.cloned.1.call-update) | async-done | bytes 2320
  968.1 22.2 %all-reduce.4 = (f32[288]{0:T(512)}, f32[96]{0:T(128)}, f32[384]{0:T(512)}, f32[96]{0:T(128)}, f32[96]{0:T(128)}, /*index=5*/f32[96]{0:T(128)}, f32[96]{0:T(128)}, f32[96]{0:T(128)}) all-reduce(f32[288]{0:T(512)S(1)} %convert_reduce_fusion, f32[96]{0:T(128)S(1)} %bitcast.113, ...), channel_id=1, replica_groups=mesh['dp'=8,'col'=4] {'dp'}, use_global_device_ids=true, to_apply=%region_19.20 | all-reduce | flops 1248 | bytes 9984 | tf_op jit(solution)/shard_map/psum | solution.py:242
  (134 shorter events, 73.4 us)
Async XLA Ops:
  7.2 4.9 copy-start.16
  7.2 45.8 %copy-start.25 = (f32[288]{0:T(512)S(1)}, f32[288]{0:T(512)}, u32[]{:S(2)}) copy-start(f32[288]{0:T(512)} %param.16) | copy-start | bytes 3460
  7.2 45.8 %all-gather.5.cloned.1.call-start = ((), (), s32[]{:S(2)}) async-start(), calls=%async_computation.12 | async-start | bytes 6051840 | tf_op jit(solution)/shard_map/all_gather | solution.py:57
  9.1 3.0 copy-start.12
  9.1 3.0 copy-start.14
  44.7 14.6 %copy-start.10 = (bf16[384,288]{1,0:T(8,128)(2,1)}, bf16[384,288]{1,0:T(8,128)(2,1)S(1)}, u32[]{:S(2)}) copy-start(bf16[384,288]{1,0:T(8,128)(2,1)S(1)} %all_gather.25) | copy-start | bytes 663556
  80.3 2.1 copy-start.2
  84.3 27.8 %collective-permute-start = (bf16[1,1,8,197,288]{3,4,0,2,1:T(8,128)(2,1)}, bf16[1,1,8,197,288]{3,4,0,2,1:T(8,128)(2,1)}, u32[]{:S(2)}, u32[]{:S(2)}) collective-permute-start(bf16[1,1,8,197,288]{3,4,0,2,1:T(8,128)(2,1)} %get-tuple-element.38), channel_id=1, source_target_pairs={{0,1},{1,2},{2,3},{3,0},{4,5},{5,6},{6,7},{7,4},{8,9},{9,10},{10,1... | collective-permute-start | bytes 2723336 | tf_op jit(solution)/shard_map/ppermute | solution.py:32
  84.5 30.0 %collective-permute-start.1 = (bf16[1,1,8,197,288]{3,4,0,2,1:T(8,128)(2,1)}, bf16[1,1,8,197,288]{3,4,0,2,1:T(8,128)(2,1)S(1)}, u32[]{:S(2)}, u32[]{:S(2)}) collective-permute-start(bf16[1,1,8,197,288]{3,4,0,2,1:T(8,128)(2,1)} %get-tuple-element.37), channel_id=1, source_target_pairs={{0,2},{1,3},{2,0},{3,1},{4,6},{5,7},{6,4},{7,5},{8,10},{9,11},{10,... | collective-permute-start | bytes 2723336 | tf_op jit(solution)/shard_map/ppermute | solution.py:32
  84.8 51.1 %collective-permute-start.2 = (bf16[1,1,8,197,288]{3,4,0,2,1:T(8,128)(2,1)}, bf16[1,1,8,197,288]{3,4,0,2,1:T(8,128)(2,1)S(1)}, u32[]{:S(2)}, u32[]{:S(2)}) collective-permute-start(bf16[1,1,8,197,288]{3,4,0,2,1:T(8,128)(2,1)} %get-tuple-element.36), channel_id=1, source_target_pairs={{0,3},{1,0},{2,1},{3,2},{4,7},{5,4},{6,5},{7,6},{8,11},{9,8},{10,9... | collective-permute-start | bytes 2723336 | tf_op jit(solution)/shard_map/ppermute | solution.py:32
  154.8 5.7 copy-start.22
  156.9 34.8 %all-to-all-start = ((bf16[1,8,197,384]{2,1,0,3:T(8,128)(2,1)}), bf16[1,8,197,384]{2,1,0,3:T(8,128)(2,1)S(1)}, u32[]{:S(2)}, u32[]{:S(2)}) async-start(bf16[1,8,197,384]{2,1,0,3:T(8,128)(2,1)} %copy.93), calls=%async_computation | async-start | bytes 3145728 | tf_op jit(solution)/shard_map/all_to_all | solution.py:166
  160.4 100.6 %reduce-scatter.30.cloned.1.call-start = ((), (), s32[]{:S(2)}) async-start(), calls=%async_computation.21 | async-start | bytes 6051840
  191.6 1.1 copy-start.7
  206.7 3.8 copy-start.5
  210.5 50.6 %copy-start = (bf16[1576,384]{1,0:T(8,128)(2,1)S(1)}, bf16[1576,384]{1,0:T(8,128)(2,1)}, u32[]{:S(2)}) copy-start(bf16[1576,384]{1,0:T(8,128)(2,1)} %param.14) | copy-start | bytes 3631108
  210.5 50.6 %copy-start.19 = (f32[384]{0:T(512)S(1)}, f32[384]{0:T(512)}, u32[]{:S(2)}) copy-start(f32[384]{0:T(512)} %param.18) | copy-start | bytes 4612
  210.5 52.6 %copy-start.20 = (f32[384]{0:T(512)S(1)}, f32[384]{0:T(512)}, u32[]{:S(2)}) copy-start(f32[384]{0:T(512)} %param.25) | copy-start | bytes 4612
  210.5 52.6 %copy-start.23 = (f32[384]{0:T(512)S(1)}, f32[384]{0:T(512)}, u32[]{:S(2)}) copy-start(f32[384]{0:T(512)} %param.26) | copy-start | bytes 4612
  210.5 56.2 %copy-start.17 = (bf16[48,384]{1,0:T(8,128)(2,1)S(1)}, bf16[48,384]{1,0:T(8,128)(2,1)}, u32[]{:S(2)}) copy-start(bf16[48,384]{1,0:T(8,128)(2,1)} %param.19) | copy-start | bytes 110596
  210.5 87.2 %copy-start.18 = (bf16[384,48]{0,1:T(8,128)(2,1)S(1)}, bf16[384,48]{0,1:T(8,128)(2,1)}, u32[]{:S(2)}) copy-start(bf16[384,48]{0,1:T(8,128)(2,1)} %param.21) | copy-start | bytes 110596
  210.5 129.0 %copy-start.26 = (f32[384]{0:T(512)S(1)}, f32[384]{0:T(512)}, u32[]{:S(2)}) copy-start(f32[384]{0:T(512)} %param.20) | copy-start | bytes 4612
  210.6 129.0 %all-gather.7.cloned.1.call-start = ((), (), s32[]{:S(2)}) async-start(), calls=%async_computation.13 | async-start | bytes 6051840 | tf_op jit(solution)/shard_map/all_gather | solution.py:57
  266.1 99.9 %all-gather.9.cloned.1.call-start = ((), (), s32[]{:S(2)}) async-start(), calls=%async_computation.14 | async-start | bytes 6051840 | tf_op jit(solution)/shard_map/all_gather | solution.py:57
  266.7 165.2 %reduce-scatter.34.cloned.1.call-start = ((), (), s32[]{:S(2)}) async-start(), calls=%async_computation.23 | async-start | bytes 6051840
  375.2 2.2 copy-start.1
  382.6 100.8 %reduce-scatter.32.cloned.1.call-start = ((), (), s32[]{:S(2)}) async-start(), calls=%async_computation.22 | async-start | bytes 6051840
  390.3 41.6 %copy-start.4 = (bf16[1576,384]{1,0:T(8,128)(2,1)S(1)}, bf16[1576,384]{1,0:T(8,128)(2,1)}, u32[]{:S(2)}) copy-start(bf16[1576,384]{1,0:T(8,128)(2,1)} %reduce-scatter.30.cloned.1.call-done) | copy-start | bytes 3631108
  390.3 93.1 %copy-start.24 = (f32[384]{0:T(512)S(1)}, f32[384]{0:T(512)}, u32[]{:S(2)}) copy-start(f32[384]{0:T(512)} %param.22) | copy-start | bytes 4612
  390.3 138.7 %all-gather.11.cloned.1.call-start = ((), (), s32[]{:S(2)}) async-start(), calls=%async_computation.15 | async-start | bytes 6051840 | tf_op jit(solution)/shard_map/all_gather | solution.py:57
  488.0 1.4 copy-start.3
  541.3 23.6 %all-to-all-start.1 = ((bf16[4,8,197,96]{2,1,3,0:T(8,128)(2,1)}), bf16[4,8,197,96]{2,1,3,0:T(8,128)(2,1)S(1)}, u32[]{:S(2)}, u32[]{:S(2)}) async-start(bf16[4,8,197,96]{2,1,3,0:T(8,128)(2,1)} %copy.96), calls=%async_computation.1 | async-start | bytes 3145728 | tf_op jit(solution)/shard_map/all_to_all | solution.py:203
  566.4 11.7 %copy-start.8 = (bf16[1,8,197,4,96]{2,4,3,1,0:T(8,128)(2,1)S(1)}, bf16[1,8,197,4,96]{2,4,3,1,0:T(8,128)(2,1)}, u32[]{:S(2)}) copy-start(bf16[1,8,197,4,96]{2,4,3,1,0:T(8,128)(2,1)} %copy.97) | copy-start | bytes 3631108
  601.3 16.9 %copy-start.9 = (bf16[8,197,1,6,64]{1,4,3,0,2:T(8,128)(2,1)S(1)}, bf16[8,197,1,6,64]{1,4,3,0,2:T(8,128)(2,1)}, u32[]{:S(2)}) copy-start(bf16[8,197,1,6,64]{1,4,3,0,2:T(8,128)(2,1)} %fusion.79) | copy-start | bytes 3631108
  634.3 58.8 %all-to-all-start.2 = ((bf16[1,8,197,1152]{2,1,0,3:T(8,128)(2,1)}), bf16[1,8,197,1152]{2,1,0,3:T(8,128)(2,1)}, u32[]{:S(2)}, u32[]{:S(2)}) async-start(bf16[1,8,197,1152]{2,1,0,3:T(8,128)(2,1)} %copy.102), calls=%async_computation.2 | async-start | bytes 9437184 | tf_op jit(solution)/shard_map/all_to_all | solution.py:207
  639.3 105.2 %reduce-scatter.26.cloned.1.call-start = ((), (), s32[]{:S(2)}) async-start(), calls=%async_computation.19 | async-start | bytes 331776 | tf_op jit(solution)/shard_map/reduce_scatter | solution.py:238
  646.7 7.7 copy-start.6
  646.7 122.9 %reduce-scatter.24.cloned.1.call-start = ((), (), s32[]{:S(2)}) async-start(), calls=%async_computation.18 | async-start | bytes 331776 | tf_op jit(solution)/shard_map/reduce_scatter | solution.py:235
  654.3 176.1 %reduce-scatter.22.cloned.1.call-start = ((), (), s32[]{:S(2)}) async-start(), calls=%async_computation.17 | async-start | bytes 110592 | tf_op jit(solution)/shard_map/reduce_scatter | solution.py:232
  659.5 232.8 %reduce-scatter.20.cloned.1.call-start = ((), (), s32[]{:S(2)}) async-start(), calls=%async_computation.16 | async-start | bytes 331776 | tf_op jit(solution)/shard_map/reduce_scatter | solution.py:229
  729.6 7.4 copy-start.11
  736.6 206.3 %reduce-scatter.36.cloned.1.call-start = ((), (), s32[]{:S(2)}) async-start(), calls=%async_computation.24 | async-start | bytes 6051840
  744.4 198.5 %copy-start.13 = (f32[1576]{0:T(1024)S(1)}, f32[1576]{0:T(1024)}, u32[]{:S(2)}) copy-start(f32[1576]{0:T(1024)} %copy-done.12) | copy-start | bytes 18916
  744.4 198.5 %copy-start.15 = (f32[1576]{0:T(1024)S(1)}, f32[1576]{0:T(1024)}, u32[]{:S(2)}) copy-start(f32[1576]{0:T(1024)} %copy-done.14) | copy-start | bytes 18916
  744.4 198.5 %copy-start.21 = (f32[384]{0:T(512)S(1)}, f32[384]{0:T(512)}, u32[]{:S(2)}) copy-start(f32[384]{0:T(512)} %param.23) | copy-start | bytes 4612
  744.5 222.0 %reduce-scatter.28.cloned.1.call-start = ((), (), s32[]{:S(2)}) async-start(), calls=%async_computation.20 | async-start | bytes 245760
Sparse Core Ops, SparseCore 0:
  12.1 40.8 all-gather.4
  210.6 50.3 reduce-scatter.29
  266.2 38.1 all-gather.6
  305.8 38.1 all-gather.8
  382.7 49.1 reduce-scatter.33
  434.3 49.0 reduce-scatter.31
  490.8 38.1 all-gather.10
  646.8 60.8 reduce-scatter.25
  711.0 58.5 reduce-scatter.23
  772.7 57.7 reduce-scatter.21
  833.7 58.5 reduce-scatter.19
  894.7 48.1 reduce-scatter.35
  946.6 19.7 reduce-scatter.27
